TPU v7x, 256 devices: a 4x2x16 block of a 4x16x16 slice. The times are simulated.
256 devices in a mesh: groups: 2 (over y), ctx: 16 (over z), fsdp: 8 (over x, core).
Axes of the slice: x: 4, y: 2, z: 16, core: 2. Of those that a mesh axis runs over, the one named last changes fastest.
The devices are a block of a 4x16x16 slice.
Arguments:
- patches: bfloat16 [16, 4096, 1024], P(('groups', 'fsdp'), 'ctx'), parts along dimension 0, may hold values from -6 to 6
- segment_ids: int32 [16, 4096], P(('groups', 'fsdp'), 'ctx'), parts along dimension 0, may hold values from 0 to 15, never falling along the last dimension, each value on 1 to 3072 neighbouring positions
- patch_rows: int32 [16, 4096], P(('groups', 'fsdp'), 'ctx'), parts along dimension 0, may hold values from 0 to 63
- patch_cols: int32 [16, 4096], P(('groups', 'fsdp'), 'ctx'), parts along dimension 0, may hold values from 0 to 63
- row_table: bfloat16 [64, 1024], replicated, may hold values from -3 to 3
- col_table: bfloat16 [64, 1024], replicated, may hold values from -3 to 3
- norm_gain: float32 [1024], replicated, may hold values from 0.1 to 1.9
- qkv_weight: bfloat16 [1024, 3072], P('fsdp'), may hold values from -5 to 5
- out_weight: bfloat16 [1024, 1024], P(None, 'fsdp'), may hold values from -0.1875 to 0.1875
Outputs:
- encoded: bfloat16 [16, 4096, 1024], P(('groups', 'fsdp'), 'ctx'), parts along dimension 0
There are 2 independent parts, one for each index of `groups`. A program takes and returns all parts, laid end to end along the dimension named above; an argument that names none is the same for every part. Nothing has to cross between parts.
All inputs are finite; a program needn't handle non-finite values.
Results may differ from a plain program's by a relative error of at most 0.0044.
The roundings to bfloat16 on the way count: a program that leaves them out, or rounds other values in their place, can miss the bound.
Values may be sent and summed in bfloat16 or wider, within the bound.
A program may use at most 64 MiB of HBM per device.

v0:
```python
import jax
import jax.numpy as jnp
from jax import lax
from jax.sharding import Mesh
from jax.sharding import PartitionSpec as P

HEADS = 16
FSDP = ("fsdp_0", "fsdp_1")
GROUPS_FSDP = ("groups", "fsdp_0", "fsdp_1")
floor_score = -1e30
epsilon = 1e-06


def laid_out(blocks, dim):
    lengths = list(blocks.shape[1:])
    lengths[dim] *= blocks.shape[0]
    return jnp.moveaxis(blocks, 0, dim).reshape(lengths)


def sent_to_all(value, axis):
    copies = jnp.broadcast_to(value, (lax.axis_size(axis), *value.shape))
    return lax.all_to_all(copies, axis, split_axis=0, concat_axis=0, tiled=True)


def collect(value, axis, dim):
    return laid_out(sent_to_all(value, axis), dim)


def edges_of(length, count):
    unit = 8 if length >= 8 * count else 1
    return [length // unit * k // count * unit for k in range(1, count)]


def stacked_from(value, axes, order):
    blocks = value[None]
    for k in order:
        blocks = lax.all_gather(blocks, axes[k], axis=0, tiled=True)
    block = [lax.axis_size(axes[k]) for k in reversed(order)]
    blocks = blocks.reshape(*block, *value.shape)
    turned = sorted(range(len(order)), key=lambda place: order[len(order) - 1 - place])
    return blocks.transpose(*turned, *range(len(order), blocks.ndim)).reshape(-1, *value.shape)


def spread_gather(value, axes, dim):
    cut = max(range(max(1, value.ndim - 1)), key=lambda d: value.shape[d])
    count, done = (len(axes), [])
    for initial, section in enumerate(
        jnp.split(value, edges_of(value.shape[cut], count), axis=cut)
    ):
        if section.size:
            order = [(initial - k) % count for k in range(count)]
            done.append(stacked_from(section, axes, order))
    return laid_out(jnp.concatenate(done, axis=cut + 1), dim)


def body(
    patches,
    segment_ids,
    patch_rows,
    patch_cols,
    row_table,
    col_table,
    norm_gain,
    qkv_weight,
    out_weight,
):
    tokens = patches[0]
    labels = segment_ids[0]
    model_width = tokens.shape[1]
    head_count = HEADS
    head_size = model_width // head_count
    score_scale = 1.0 / head_size**0.5
    grid_size = row_table.shape[0]
    levels = lax.broadcasted_iota(jnp.int32, (1, grid_size), 1)
    row_onehot = (patch_rows[0][:, None] == levels).astype(jnp.bfloat16)
    col_onehot = (patch_cols[0][:, None] == levels).astype(jnp.bfloat16)
    embedded = (
        tokens.astype(jnp.float32)
        + jnp.dot(row_onehot, row_table, preferred_element_type=jnp.float32)
        + jnp.dot(col_onehot, col_table, preferred_element_type=jnp.float32)
    )
    average = jnp.mean(embedded, axis=-1, keepdims=True)
    centered = embedded - average
    variance = jnp.mean(centered * centered, axis=-1, keepdims=True)
    normed = (centered * lax.rsqrt(variance + epsilon) * norm_gain).astype(jnp.bfloat16)
    qkv = jnp.dot(
        normed,
        lax.all_gather(qkv_weight, FSDP, axis=0, tiled=True),
        preferred_element_type=jnp.float32,
    ).astype(jnp.bfloat16)
    queries = qkv[:, :model_width]
    key_rows = qkv[:, model_width : 2 * model_width]
    value_rows = qkv[:, 2 * model_width :]
    query_part, key_part, value_part = (
        lax.all_to_all(queries, "ctx", split_axis=1, concat_axis=0, tiled=True),
        lax.all_to_all(key_rows, "ctx", split_axis=1, concat_axis=0, tiled=True),
        lax.all_to_all(value_rows, "ctx", split_axis=1, concat_axis=0, tiled=True),
    )
    full_labels = collect(labels, "ctx", 0)
    full_length = query_part.shape[0]
    local_width = query_part.shape[1]
    local_heads = local_width // head_size
    span = min(512, full_length)
    key_heads = key_part.reshape(full_length, local_heads, head_size)
    value_heads = value_part.reshape(full_length, local_heads, head_size)

    def attend_span(offset):
        span_rows = lax.dynamic_slice_in_dim(query_part, offset, span, 0).reshape(
            span, local_heads, head_size
        )
        span_labels = lax.dynamic_slice_in_dim(full_labels, offset, span, 0)
        scores = (
            jnp.einsum("qhd,khd->hqk", span_rows, key_heads, preferred_element_type=jnp.float32)
            * score_scale
        )
        same_segment = (span_labels[:, None] == full_labels[None, :])[None]
        masked = jnp.where(same_segment, scores, floor_score)
        highest = jnp.max(masked, axis=-1, keepdims=True)
        raised = jnp.where(same_segment, jnp.exp(masked - highest), 0.0)
        row_sums = jnp.sum(raised, axis=-1)
        mixed = jnp.einsum(
            "hqk,khd->qhd",
            raised.astype(jnp.bfloat16),
            value_heads,
            preferred_element_type=jnp.float32,
        )
        mixed = mixed / row_sums.T[:, :, None]
        return mixed.reshape(span, local_width).astype(jnp.bfloat16)

    offsets = jnp.arange(full_length // span, dtype=jnp.int32) * span
    head_context = lax.map(attend_span, offsets).reshape(full_length, local_width)
    context = lax.all_to_all(head_context, "ctx", split_axis=0, concat_axis=1, tiled=True)
    attended = jnp.dot(
        context, spread_gather(out_weight, FSDP, 1), preferred_element_type=jnp.float32
    )
    encoded = (embedded + attended).astype(jnp.bfloat16)
    return encoded[None]


def solution(mesh):
    finer = Mesh(
        mesh.devices.reshape(mesh.shape["groups"], mesh.shape["ctx"], 4, 2),
        ("groups", "ctx", "fsdp_0", "fsdp_1"),
    )
    placed = (
        P(GROUPS_FSDP, "ctx", None),
        P(GROUPS_FSDP, "ctx"),
        P(GROUPS_FSDP, "ctx"),
        P(GROUPS_FSDP, "ctx"),
        P(),
        P(),
        P(),
        P(FSDP, None),
        P(None, FSDP),
    )
    return jax.shard_map(
        body, mesh=finer, in_specs=placed, out_specs=P(GROUPS_FSDP, "ctx", None), check_vma=False
    )
```

profile of v0, /device:TPU:40, one launch (start us, length us, event | category | flops | bytes accessed | tf_op | source)
XLA Modules:
  0.0 326.7 jit_solution(15467032216599425548)
XLA Ops:
  9.5 24.0 %all-to-all-start = ((s32[16,1,256]{2,1,0:T(1,128)}), s32[16,1,256]{2,1,0:T(1,128)S(1)}, u32[]{:S(2)}, u32[]{:S(2)}) async-start(s32[16,1,256]{2,1,0:T(1,128)} %broadcast_in_dim.31), calls=%async_computation | async-start | bytes 32768 | tf_op jit(solution)/shard_map/all_to_all | solution.py:22
  36.3 33.9 %all-gather.6.cloned.1.call-done = bf16[1024,3072]{1,0:T(8,128)(2,1)} async-done(((bf16[128,3072]{1,0:T(8,128)(2,1)}), bf16[1024,3072]{1,0:T(8,128)(2,1)}) %all-gather.6.cloned.1.call-update) | async-done | bytes 6291472 | tf_op jit(solution)/shard_map/all_gather | solution.py:88
  70.2 4.7 %convolution_convert_fusion = bf16[256,3072]{1,0:T(8,128)(2,1)S(1)} fusion(bf16[1024,3072]{1,0:T(8,128)(2,1)} %all-gather.6.cloned.1.call-done, f32[256,1024]{1,0:T(8,128)S(1)} %get-tuple-element.96, f32[1024]{0:T(1024)} %param.17, f32[256]{0:T(256)S(1)} %add_rsqrt_fusion, f32[256]{0:T(256)S(1)} %broadcast_multiply_fusion), kind=kOutput, calls=%fused_computation.19 | convolution fusion | flops 1612447744 | bytes 8919040 | tf_op jit(solution)/shard_map/dot_general | solution.py:86
  76.1 12.4 %all-to-all-start.1 = ((bf16[256,16,64]{0,2,1:T(8,128)(2,1)}), bf16[256,16,64]{0,2,1:T(8,128)(2,1)S(1)}, u32[]{:S(2)}, u32[]{:S(2)}) async-start(bf16[256,16,64]{0,2,1:T(8,128)(2,1)} %bitcast.12), calls=%async_computation.1 | async-start | bytes 1048576 | tf_op jit(solution)/shard_map/all_to_all | solution.py:95
  89.4 28.0 %all-to-all-done.1 = bf16[256,16,64]{0,2,1:T(8,128)(2,1)S(1)} async-done(((bf16[256,16,64]{0,2,1:T(8,128)(2,1)}), bf16[256,16,64]{0,2,1:T(8,128)(2,1)S(1)}, u32[]{:S(2)}, u32[]{:S(2)}) %all-to-all-start.1) | async-done | bytes 524320 | tf_op jit(solution)/shard_map/all_to_all | solution.py:95
  117.5 6.8 %all-to-all-start.2 = ((bf16[256,16,64]{0,2,1:T(8,128)(2,1)}), bf16[256,16,64]{0,2,1:T(8,128)(2,1)S(1)}, u32[]{:S(2)}, u32[]{:S(2)}) async-start(bf16[256,16,64]{0,2,1:T(8,128)(2,1)} %bitcast.15), calls=%async_computation.2 | async-start | bytes 1048576 | tf_op jit(solution)/shard_map/all_to_all | solution.py:96
  125.3 27.9 %all-to-all-done.2 = bf16[256,16,64]{0,2,1:T(8,128)(2,1)S(1)} async-done(((bf16[256,16,64]{0,2,1:T(8,128)(2,1)}), bf16[256,16,64]{0,2,1:T(8,128)(2,1)S(1)}, u32[]{:S(2)}, u32[]{:S(2)}) %all-to-all-start.2) | async-done | bytes 524320 | tf_op jit(solution)/shard_map/all_to_all | solution.py:96
  153.2 6.6 %all-to-all-start.3 = ((bf16[256,16,64]{0,2,1:T(8,128)(2,1)}), bf16[256,16,64]{0,2,1:T(8,128)(2,1)S(1)}, u32[]{:S(2)}, u32[]{:S(2)}) async-start(bf16[256,16,64]{0,2,1:T(8,128)(2,1)} %bitcast.17), calls=%async_computation.3 | async-start | bytes 1048576 | tf_op jit(solution)/shard_map/all_to_all | solution.py:97
  160.0 14.4 %all-gather = bf16[2048,128]{1,0:T(8,128)(2,1)} all-gather(bf16[512,128]{1,0:T(8,128)(2,1)S(1)} %get-tuple-element.93), channel_id=2, replica_groups=mesh['groups'=2,'ctx'=16,'fsdp_0'=4,'fsdp_1'=2] {'fsdp_0'}, dimensions={0}, use_global_device_ids=true | all-gather | bytes 655360 | tf_op jit(solution)/shard_map/all_gather | solution.py:37
  176.3 12.4 %all-to-all-done.3 = bf16[256,16,64]{0,2,1:T(8,128)(2,1)S(1)} async-done(((bf16[256,16,64]{0,2,1:T(8,128)(2,1)}), bf16[256,16,64]{0,2,1:T(8,128)(2,1)S(1)}, u32[]{:S(2)}, u32[]{:S(2)}) %all-to-all-start.3) | async-done | bytes 524320 | tf_op jit(solution)/shard_map/all_to_all | solution.py:97
  189.3 81.4 %while.10 = (s32[]{:T(128)}, bf16[8,512,64]{1,2,0:T(8,128)(2,1)S(1)}, s32[8]{0:T(128)S(1)}, s32[4096]{0:T(1024)S(1)}, s32[16,256]{1,0:T(8,128)S(1)}, /*index=5*/...) while((s32[]{:T(128)}, ...), condition=%wide.region_5.6_spmd, body=%wide.region_2.5_spmd.sunk | while | flops 570489856 | bytes 26513576 | solution.py:131
  194.4 2.6 fusion.51
  197.0 2.5 fusion.52
  204.6 2.6 fusion.51
  207.2 2.5 fusion.52
  214.8 2.6 fusion.51
  217.3 2.5 fusion.52
  224.9 2.6 fusion.51
  227.5 2.5 fusion.52
  235.1 2.6 fusion.51
  237.7 2.5 fusion.52
  245.3 2.6 fusion.51
  247.9 2.5 fusion.52
  255.4 2.6 fusion.51
  258.0 2.5 fusion.52
  265.6 2.6 fusion.51
  268.2 2.5 fusion.52
  272.2 6.7 %all-to-all-start.4 = ((bf16[16,256,64]{1,2,0:T(8,128)(2,1)}), bf16[16,256,64]{1,2,0:T(8,128)(2,1)}, u32[]{:S(2)}, u32[]{:S(2)}) async-start(bf16[16,256,64]{1,2,0:T(8,128)(2,1)} %copy.50), calls=%async_computation.4 | async-start | bytes 1048576 | tf_op jit(solution)/shard_map/all_to_all | solution.py:132
  282.5 28.6 %all-gather.10.cloned.1.call-done = bf16[8,512,128]{2,1,0:T(8,128)(2,1)} async-done(((bf16[2,512,128]{2,1,0:T(8,128)(2,1)}), bf16[8,512,128]{2,1,0:T(8,128)(2,1)}) %all-gather.10.cloned.1.call-update) | async-done | bytes 1048592 | tf_op jit(solution)/shard_map/all_gather | solution.py:37
  311.0 2.7 maximum_bitcast_fusion
  313.8 2.9 copy.52
  316.6 2.6 fusion.29
  (69 shorter events, 40.6 us)
Async XLA Ops:
  7.4 27.5 %copy-start = (bf16[64,1024]{1,0:T(8,128)(2,1)S(1)}, bf16[64,1024]{1,0:T(8,128)(2,1)}, u32[]{:S(2)}) copy-start(bf16[64,1024]{1,0:T(8,128)(2,1)} %param.16) | copy-start | bytes 393220
  7.4 62.8 %all-gather.6.cloned.1.call-start = ((), (), s32[]{:S(2)}) async-start(), calls=%async_computation.5 | async-start | bytes 7077888 | tf_op jit(solution)/shard_map/all_gather | solution.py:88
  9.5 66.6 %all-to-all-start = ((s32[16,1,256]{2,1,0:T(1,128)}), s32[16,1,256]{2,1,0:T(1,128)S(1)}, u32[]{:S(2)}, u32[]{:S(2)}) async-start(s32[16,1,256]{2,1,0:T(1,128)} %broadcast_in_dim.31), calls=%async_computation | async-start | bytes 32768 | tf_op jit(solution)/shard_map/all_to_all | solution.py:22
  74.9 85.0 %copy-start.1 = (bf16[1024,128]{1,0:T(8,128)(2,1)S(1)}, bf16[1024,128]{1,0:T(8,128)(2,1)}, u32[]{:S(2)}) copy-start(bf16[1024,128]{1,0:T(8,128)(2,1)} %param.19) | copy-start | bytes 786436
  76.1 41.4 %all-to-all-start.1 = ((bf16[256,16,64]{0,2,1:T(8,128)(2,1)}), bf16[256,16,64]{0,2,1:T(8,128)(2,1)S(1)}, u32[]{:S(2)}, u32[]{:S(2)}) async-start(bf16[256,16,64]{0,2,1:T(8,128)(2,1)} %bitcast.12), calls=%async_computation.1 | async-start | bytes 1048576 | tf_op jit(solution)/shard_map/all_to_all | solution.py:95
  117.5 35.7 %all-to-all-start.2 = ((bf16[256,16,64]{0,2,1:T(8,128)(2,1)}), bf16[256,16,64]{0,2,1:T(8,128)(2,1)S(1)}, u32[]{:S(2)}, u32[]{:S(2)}) async-start(bf16[256,16,64]{0,2,1:T(8,128)(2,1)} %bitcast.15), calls=%async_computation.2 | async-start | bytes 1048576 | tf_op jit(solution)/shard_map/all_to_all | solution.py:96
  153.2 35.6 %all-to-all-start.3 = ((bf16[256,16,64]{0,2,1:T(8,128)(2,1)}), bf16[256,16,64]{0,2,1:T(8,128)(2,1)S(1)}, u32[]{:S(2)}, u32[]{:S(2)}) async-start(bf16[256,16,64]{0,2,1:T(8,128)(2,1)} %bitcast.17), calls=%async_computation.3 | async-start | bytes 1048576 | tf_op jit(solution)/shard_map/all_to_all | solution.py:97
  159.8 121.3 %all-gather.8.cloned.1.call-start = ((), (), s32[]{:S(2)}) async-start(), calls=%async_computation.6 | async-start | bytes 1572864 | tf_op jit(solution)/shard_map/all_gather | solution.py:37
  272.2 44.5 %all-to-all-start.4 = ((bf16[16,256,64]{1,2,0:T(8,128)(2,1)}), bf16[16,256,64]{1,2,0:T(8,128)(2,1)}, u32[]{:S(2)}, u32[]{:S(2)}) async-start(bf16[16,256,64]{1,2,0:T(8,128)(2,1)} %copy.50), calls=%async_computation.4 | async-start | bytes 1048576 | tf_op jit(solution)/shard_map/all_to_all | solution.py:132
  278.8 32.2 %all-gather.10.cloned.1.call-start = ((), (), s32[]{:S(2)}) async-start(), calls=%async_computation.7 | async-start | bytes 1310720 | tf_op jit(solution)/shard_map/all_gather | solution.py:37
Sparse Core Ops, SparseCore 0:
  10.1 60.1 all-gather.5
Sparse Core Ops, SparseCore 1:
  174.5 17.2 all-gather.7
  281.2 29.8 all-gather.9
where the time goes:
time: 328 us; the launch traced here: 327 us
  waiting for transfers between devices  132 us (40%)
  starting transfers between devices  56.5 us (17%)
  matrix products  49.5 us (15%)
  other arithmetic  23.6 us (7%)
  local copies, waits for them, and re-layouts  17.8 us (5%)
  blocking collectives  16.6 us (5%)
  loops' own time  15.8 us (5%)
  between operations  15.1 us (5%)
    all_gather x1, waiting for transfers between devices, body(): lax.all_gather(qkv_weight, FSDP, axis=0, tiled=True)  33.9 us
    all_gather x2, waiting for transfers between devices, stacked_from(): blocks = lax.all_gather(blocks, axes[k], axis=0, tiled=True)  28.6 us
    all_to_all x1, waiting for transfers between devices, body(): lax.all_to_all(queries, 'ctx', split_axis=1, concat_axis=0, tiled=True)  28 us
    all_to_all x1, waiting for transfers between devices, body(): lax.all_to_all(key_rows, 'ctx', split_axis=1, concat_axis=0, tiled=True)  27.9 us
    all_to_all x1, starting transfers between devices, sent_to_all(): return lax.all_to_all(copies, axis, split_axis=0, concat_axis=0, tiled=True)  24 us
    reduce_sum x8, other arithmetic, attend_span(): row_sums = jnp.sum(raised, axis=-1)  20.6 us
    dot_general x8, matrix products, attend_span(): jnp.einsum('hqk,khd->qhd', raised.astype(jnp.bfloat16), value_heads, pref...  20.1 us
    dot_general x8, matrix products, attend_span(): jnp.einsum('qhd,khd->hqk', span_rows, key_heads, preferred_element_type=j...  19.5 us
  transfers between devices with their start and end apart: 8, of which 5 were waited for; matrix products, arithmetic and copies ran while one was open for 27% of the time, Pallas kernels for 0%

commit v1 on v0

--- a/solution.py
+++ b/solution.py
@@ -1,3 +1,4 @@
+import functools
 import jax
 import jax.numpy as jnp
 from jax import lax
@@ -9,6 +10,21 @@
 GROUPS_FSDP = ("groups", "fsdp_0", "fsdp_1")
 floor_score = -1e30
 epsilon = 1e-06
+
+
+def detail_axis_part(target, mesh_dim):
+    return jnp.concatenate(
+        lax.all_to_all(
+            jnp.stack([target for _ in range(lax.axis_size(mesh_dim))]),
+            mesh_dim,
+            split_axis=0,
+            concat_axis=0,
+        ),
+        axis=0,
+    )
+
+
+register_plane = functools.partial(detail_axis_part, mesh_dim=FSDP)
 
 
 def laid_out(blocks, dim):
@@ -83,11 +99,9 @@
     centered = embedded - average
     variance = jnp.mean(centered * centered, axis=-1, keepdims=True)
     normed = (centered * lax.rsqrt(variance + epsilon) * norm_gain).astype(jnp.bfloat16)
-    qkv = jnp.dot(
-        normed,
-        lax.all_gather(qkv_weight, FSDP, axis=0, tiled=True),
-        preferred_element_type=jnp.float32,
-    ).astype(jnp.bfloat16)
+    qkv = jnp.dot(normed, register_plane(qkv_weight), preferred_element_type=jnp.float32).astype(
+        jnp.bfloat16
+    )
     queries = qkv[:, :model_width]
     key_rows = qkv[:, model_width : 2 * model_width]
     value_rows = qkv[:, 2 * model_width :]

time: 328 us -> 367 us (1.12)
  waiting for transfers between devices: 132 us -> 172 us
  local copies, waits for them, and re-layouts: 17.8 us -> 21.8 us
    all_to_all x0 -> x1, waiting for transfers between devices: none -> 70.9 us  [detail_axis_part(): lax.all_to_all(jnp.stack([target for _ in range(lax.axis_size(mesh_dim))]...]
    all_gather x1 -> x0, waiting for transfers between devices: 33.9 us -> none  [body(): lax.all_gather(qkv_weight, FSDP, axis=0, tiled=True)]
    all_to_all x1, starting transfers between devices: 12.4 us -> 5.56 us  [body(): lax.all_to_all(queries, 'ctx', split_axis=1, concat_axis=0, tiled=True)]
    all_to_all x1, waiting for transfers between devices: 0.01 us -> 6.48 us  [sent_to_all(): return lax.all_to_all(copies, axis, split_axis=0, concat_axis=0, tiled=True)]
    all_to_all x0 -> x1, starting transfers between devices: none -> 5.06 us  [detail_axis_part(): lax.all_to_all(jnp.stack([target for _ in range(lax.axis_size(mesh_dim))]...]
    another operation x0 -> x1, local copies, waits for them, and re-layouts: none -> 4.66 us  [detail_axis_part(): jnp.stack([target for _ in range(lax.axis_size(mesh_dim))])]
  transfers between devices with their start and end apart: 8 -> 8, of which waited for: 5 -> 6; matrix products, arithmetic and copies ran while one was open for 27% -> 23% of each run, Pallas kernels for 0% -> 0%
where the time goes in v1:
time: 367 us; the launch traced here: 366 us
  waiting for transfers between devices  172 us (47%)
  starting transfers between devices  54.9 us (15%)
  matrix products  47.7 us (13%)
  other arithmetic  23.6 us (6%)
  local copies, waits for them, and re-layouts  21.8 us (6%)
  blocking collectives  16.6 us (5%)
  loops' own time  15.8 us (4%)
  between operations  13.7 us (4%)
    all_to_all x1, waiting for transfers between devices, detail_axis_part(): lax.all_to_all(jnp.stack([target for _ in range(lax.axis_size(mesh_dim))]...  70.9 us
    all_gather x2, waiting for transfers between devices, stacked_from(): blocks = lax.all_gather(blocks, axes[k], axis=0, tiled=True)  28.3 us
    all_to_all x1, waiting for transfers between devices, body(): lax.all_to_all(key_rows, 'ctx', split_axis=1, concat_axis=0, tiled=True)  27.4 us
    all_to_all x1, waiting for transfers between devices, body(): lax.all_to_all(queries, 'ctx', split_axis=1, concat_axis=0, tiled=True)  26.7 us
    all_to_all x1, starting transfers between devices, sent_to_all(): return lax.all_to_all(copies, axis, split_axis=0, concat_axis=0, tiled=True)  24 us
    reduce_sum x8, other arithmetic, attend_span(): row_sums = jnp.sum(raised, axis=-1)  20.6 us
    dot_general x8, matrix products, attend_span(): jnp.einsum('hqk,khd->qhd', raised.astype(jnp.bfloat16), value_heads, pref...  20.1 us
    dot_general x8, matrix products, attend_span(): jnp.einsum('qhd,khd->hqk', span_rows, key_heads, preferred_element_type=j...  19.6 us
  transfers between devices with their start and end apart: 8, of which 6 were waited for; matrix products, arithmetic and copies ran while one was open for 23% of the time, Pallas kernels for 0%

profile of v1, /device:TPU:40, one launch (start us, length us, event | category | flops | bytes accessed | tf_op | source)
XLA Modules:
  0.0 365.8 jit_solution(1661031329398723167)
XLA Ops:
  6.6 4.7 %stack.2 = bf16[8,128,3072]{2,1,0:T(8,128)(2,1)} broadcast(bf16[128,3072]{1,0:T(8,128)(2,1)} %param.18), dimensions={1,2} | broadcast | bytes 7077888 | tf_op jit(solution)/shard_map/stack | solution.py:18
  11.2 5.1 %all-to-all-start.1 = ((bf16[8,128,3072]{2,1,0:T(8,128)(2,1)}), bf16[8,128,3072]{2,1,0:T(8,128)(2,1)}, u32[]{:S(2)}, u32[]{:S(2)}) async-start(bf16[8,128,3072]{2,1,0:T(8,128)(2,1)} %stack.2), calls=%async_computation.1 | async-start | bytes 12582912 | tf_op jit(solution)/shard_map/all_to_all | solution.py:17
  17.4 70.9 %all-to-all-done.1 = bf16[8,128,3072]{2,1,0:T(8,128)(2,1)} async-done(((bf16[8,128,3072]{2,1,0:T(8,128)(2,1)}), bf16[8,128,3072]{2,1,0:T(8,128)(2,1)}, u32[]{:S(2)}, u32[]{:S(2)}) %all-to-all-start.1) | async-done | bytes 6291488 | tf_op jit(solution)/shard_map/all_to_all | solution.py:17
  88.9 24.0 %all-to-all-start = ((s32[16,1,256]{2,1,0:T(1,128)}), s32[16,1,256]{2,1,0:T(1,128)S(1)}, u32[]{:S(2)}, u32[]{:S(2)}) async-start(s32[16,1,256]{2,1,0:T(1,128)} %broadcast_in_dim.31), calls=%async_computation | async-start | bytes 32768 | tf_op jit(solution)/shard_map/all_to_all | solution.py:38
  112.9 4.7 %convolution_convert_fusion = bf16[256,3072]{1,0:T(8,128)(2,1)S(1)} fusion(bf16[1024,3072]{1,0:T(8,128)(2,1)} %bitcast.12, f32[256,1024]{1,0:T(8,128)S(1)} %get-tuple-element.96, f32[1024]{0:T(1024)S(1)} %copy-done.7, f32[256]{0:T(256)S(1)} %add_rsqrt_fusion, f32[256]{0:T(256)S(1)} %broadcast_multiply_fusion), kind=kOutput, calls=%fused_computation.19 | convolution fusion | flops 1612447744 | bytes 8919040 | tf_op jit(solution)/shard_map/dot_general | solution.py:102
  118.7 6.5 %all-to-all-done = s32[16,1,256]{2,1,0:T(1,128)S(1)} async-done(((s32[16,1,256]{2,1,0:T(1,128)}), s32[16,1,256]{2,1,0:T(1,128)S(1)}, u32[]{:S(2)}, u32[]{:S(2)}) %all-to-all-start) | async-done | bytes 16416 | tf_op jit(solution)/shard_map/all_to_all | solution.py:38
  125.2 5.6 %all-to-all-start.2 = ((bf16[256,16,64]{0,2,1:T(8,128)(2,1)}), bf16[256,16,64]{0,2,1:T(8,128)(2,1)S(1)}, u32[]{:S(2)}, u32[]{:S(2)}) async-start(bf16[256,16,64]{0,2,1:T(8,128)(2,1)} %bitcast.13), calls=%async_computation.2 | async-start | bytes 1048576 | tf_op jit(solution)/shard_map/all_to_all | solution.py:109
  131.8 26.7 %all-to-all-done.2 = bf16[256,16,64]{0,2,1:T(8,128)(2,1)S(1)} async-done(((bf16[256,16,64]{0,2,1:T(8,128)(2,1)}), bf16[256,16,64]{0,2,1:T(8,128)(2,1)S(1)}, u32[]{:S(2)}, u32[]{:S(2)}) %all-to-all-start.2) | async-done | bytes 524320 | tf_op jit(solution)/shard_map/all_to_all | solution.py:109
  158.5 6.8 %all-to-all-start.3 = ((bf16[256,16,64]{0,2,1:T(8,128)(2,1)}), bf16[256,16,64]{0,2,1:T(8,128)(2,1)S(1)}, u32[]{:S(2)}, u32[]{:S(2)}) async-start(bf16[256,16,64]{0,2,1:T(8,128)(2,1)} %bitcast.16), calls=%async_computation.3 | async-start | bytes 1048576 | tf_op jit(solution)/shard_map/all_to_all | solution.py:110
  166.3 27.4 %all-to-all-done.3 = bf16[256,16,64]{0,2,1:T(8,128)(2,1)S(1)} async-done(((bf16[256,16,64]{0,2,1:T(8,128)(2,1)}), bf16[256,16,64]{0,2,1:T(8,128)(2,1)S(1)}, u32[]{:S(2)}, u32[]{:S(2)}) %all-to-all-start.3) | async-done | bytes 524320 | tf_op jit(solution)/shard_map/all_to_all | solution.py:110
  193.8 6.6 %all-to-all-start.4 = ((bf16[256,16,64]{0,2,1:T(8,128)(2,1)}), bf16[256,16,64]{0,2,1:T(8,128)(2,1)S(1)}, u32[]{:S(2)}, u32[]{:S(2)}) async-start(bf16[256,16,64]{0,2,1:T(8,128)(2,1)} %bitcast.18), calls=%async_computation.4 | async-start | bytes 1048576 | tf_op jit(solution)/shard_map/all_to_all | solution.py:111
  200.5 14.4 %all-gather = bf16[2048,128]{1,0:T(8,128)(2,1)} all-gather(bf16[512,128]{1,0:T(8,128)(2,1)S(1)} %get-tuple-element.93), channel_id=2, replica_groups=mesh['groups'=2,'ctx'=16,'fsdp_0'=4,'fsdp_1'=2] {'fsdp_0'}, dimensions={0}, use_global_device_ids=true | all-gather | bytes 655360 | tf_op jit(solution)/shard_map/all_gather | solution.py:53
  216.9 11.8 %all-to-all-done.4 = bf16[256,16,64]{0,2,1:T(8,128)(2,1)S(1)} async-done(((bf16[256,16,64]{0,2,1:T(8,128)(2,1)}), bf16[256,16,64]{0,2,1:T(8,128)(2,1)S(1)}, u32[]{:S(2)}, u32[]{:S(2)}) %all-to-all-start.4) | async-done | bytes 524320 | tf_op jit(solution)/shard_map/all_to_all | solution.py:111
  229.3 81.4 %while.10 = (s32[]{:T(128)}, bf16[8,512,64]{1,2,0:T(8,128)(2,1)S(1)}, s32[8]{0:T(128)S(1)}, s32[4096]{0:T(1024)S(1)}, s32[16,256]{1,0:T(8,128)S(1)}, /*index=5*/...) while((s32[]{:T(128)}, ...), condition=%wide.region_5.6_spmd, body=%wide.region_2.5_spmd.sunk | while | flops 570489856 | bytes 26513576 | solution.py:145
  234.4 2.6 fusion.51
  244.5 2.6 fusion.51
  247.1 2.5 fusion.52
  254.7 2.6 fusion.51
  264.9 2.6 fusion.51
  267.5 2.5 fusion.52
  275.1 2.6 fusion.51
  277.6 2.5 fusion.52
  285.2 2.6 fusion.51
  287.8 2.5 fusion.52
  295.4 2.6 fusion.51
  298.0 2.5 fusion.52
  305.6 2.6 fusion.51
  312.1 6.7 %all-to-all-start.5 = ((bf16[16,256,64]{1,2,0:T(8,128)(2,1)}), bf16[16,256,64]{1,2,0:T(8,128)(2,1)}, u32[]{:S(2)}, u32[]{:S(2)}) async-start(bf16[16,256,64]{1,2,0:T(8,128)(2,1)} %copy.50), calls=%async_computation.5 | async-start | bytes 1048576 | tf_op jit(solution)/shard_map/all_to_all | solution.py:146
  322.5 28.3 %all-gather.7.cloned.1.call-done = bf16[8,512,128]{2,1,0:T(8,128)(2,1)} async-done(((bf16[2,512,128]{2,1,0:T(8,128)(2,1)}), bf16[8,512,128]{2,1,0:T(8,128)(2,1)}) %all-gather.7.cloned.1.call-update) | async-done | bytes 1048592 | tf_op jit(solution)/shard_map/all_gather | solution.py:53
  350.8 2.7 maximum_bitcast_fusion
  353.5 2.9 copy.52
  356.4 2.6 fusion.29
  (81 shorter events, 44.9 us)
Async XLA Ops:
  6.5 10.1 %copy-start = (bf16[64,1024]{1,0:T(8,128)(2,1)S(1)}, bf16[64,1024]{1,0:T(8,128)(2,1)}, u32[]{:S(2)}) copy-start(bf16[64,1024]{1,0:T(8,128)(2,1)} %param.16) | copy-start | bytes 393220
  6.6 9.8 %copy-start.5 = (s32[1,256]{1,0:T(1,128)S(1)}, s32[1,256]{1,0:T(1,128)}, u32[]{:S(2)}) copy-start(s32[1,256]{1,0:T(1,128)} %param.13) | copy-start | bytes 3076
  6.6 9.8 %copy-start.1 = (bf16[1,256,1024]{2,1,0:T(8,128)(2,1)S(1)}, bf16[1,256,1024]{2,1,0:T(8,128)(2,1)}, u32[]{:S(2)}) copy-start(bf16[1,256,1024]{2,1,0:T(8,128)(2,1)} %param.11) | copy-start | bytes 1572868
  6.6 9.8 %copy-start.3 = (bf16[64,1024]{1,0:T(8,128)(2,1)S(1)}, bf16[64,1024]{1,0:T(8,128)(2,1)}, u32[]{:S(2)}) copy-start(bf16[64,1024]{1,0:T(8,128)(2,1)} %param.15) | copy-start | bytes 393220
  11.2 5.5 %copy-start.4 = (s32[1,256]{1,0:T(1,128)S(1)}, s32[1,256]{1,0:T(1,128)}, u32[]{:S(2)}) copy-start(s32[1,256]{1,0:T(1,128)} %param.14) | copy-start | bytes 3076
  11.2 77.1 %copy-start.6 = (s32[1,256]{1,0:T(1,128)S(1)}, s32[1,256]{1,0:T(1,128)}, u32[]{:S(2)}) copy-start(s32[1,256]{1,0:T(1,128)} %param.12) | copy-start | bytes 3076
  11.2 101.7 %copy-start.7 = (f32[1024]{0:T(1024)S(1)}, f32[1024]{0:T(1024)}, u32[]{:S(2)}) copy-start(f32[1024]{0:T(1024)} %param.17) | copy-start | bytes 12292
  11.2 77.1 %all-to-all-start.1 = ((bf16[8,128,3072]{2,1,0:T(8,128)(2,1)}), bf16[8,128,3072]{2,1,0:T(8,128)(2,1)}, u32[]{:S(2)}, u32[]{:S(2)}) async-start(bf16[8,128,3072]{2,1,0:T(8,128)(2,1)} %stack.2), calls=%async_computation.1 | async-start | bytes 12582912 | tf_op jit(solution)/shard_map/all_to_all | solution.py:17
  88.9 36.3 %all-to-all-start = ((s32[16,1,256]{2,1,0:T(1,128)}), s32[16,1,256]{2,1,0:T(1,128)S(1)}, u32[]{:S(2)}, u32[]{:S(2)}) async-start(s32[16,1,256]{2,1,0:T(1,128)} %broadcast_in_dim.31), calls=%async_computation | async-start | bytes 32768 | tf_op jit(solution)/shard_map/all_to_all | solution.py:38
  117.6 82.9 %copy-start.2 = (bf16[1024,128]{1,0:T(8,128)(2,1)S(1)}, bf16[1024,128]{1,0:T(8,128)(2,1)}, u32[]{:S(2)}) copy-start(bf16[1024,128]{1,0:T(8,128)(2,1)} %param.19) | copy-start | bytes 786436
  125.2 33.3 %all-to-all-start.2 = ((bf16[256,16,64]{0,2,1:T(8,128)(2,1)}), bf16[256,16,64]{0,2,1:T(8,128)(2,1)S(1)}, u32[]{:S(2)}, u32[]{:S(2)}) async-start(bf16[256,16,64]{0,2,1:T(8,128)(2,1)} %bitcast.13), calls=%async_computation.2 | async-start | bytes 1048576 | tf_op jit(solution)/shard_map/all_to_all | solution.py:109
  158.5 35.3 %all-to-all-start.3 = ((bf16[256,16,64]{0,2,1:T(8,128)(2,1)}), bf16[256,16,64]{0,2,1:T(8,128)(2,1)S(1)}, u32[]{:S(2)}, u32[]{:S(2)}) async-start(bf16[256,16,64]{0,2,1:T(8,128)(2,1)} %bitcast.16), calls=%async_computation.3 | async-start | bytes 1048576 | tf_op jit(solution)/shard_map/all_to_all | solution.py:110
  193.8 35.0 %all-to-all-start.4 = ((bf16[256,16,64]{0,2,1:T(8,128)(2,1)}), bf16[256,16,64]{0,2,1:T(8,128)(2,1)S(1)}, u32[]{:S(2)}, u32[]{:S(2)}) async-start(bf16[256,16,64]{0,2,1:T(8,128)(2,1)} %bitcast.18), calls=%async_computation.4 | async-start | bytes 1048576 | tf_op jit(solution)/shard_map/all_to_all | solution.py:111
  200.4 120.8 %all-gather.5.cloned.1.call-start = ((), (), s32[]{:S(2)}) async-start(), calls=%async_computation.6 | async-start | bytes 1572864 | tf_op jit(solution)/shard_map/all_gather | solution.py:53
  312.1 44.2 %all-to-all-start.5 = ((bf16[16,256,64]{1,2,0:T(8,128)(2,1)}), bf16[16,256,64]{1,2,0:T(8,128)(2,1)}, u32[]{:S(2)}, u32[]{:S(2)}) async-start(bf16[16,256,64]{1,2,0:T(8,128)(2,1)} %copy.50), calls=%async_computation.5 | async-start | bytes 1048576 | tf_op jit(solution)/shard_map/all_to_all | solution.py:146
  318.9 32.0 %all-gather.7.cloned.1.call-start = ((), (), s32[]{:S(2)}) async-start(), calls=%async_computation.7 | async-start | bytes 1310720 | tf_op jit(solution)/shard_map/all_gather | solution.py:53
Sparse Core Ops, SparseCore 0:
  215.1 17.2 all-gather.4
  321.5 29.2 all-gather.6
